TPU v7x, 256 devices: a whole 4x4x8 slice. The times are simulated.
256 devices in a mesh: ta: 4 (over z_hi), sa: 64 (over y, z_lo, x, core).
Axes of the slice: x: 4, y: 4, z: 8 (z_hi: 4, z_lo: 2; z = z_hi * 2 + z_lo), core: 2. Of those that a mesh axis runs over, the one named last changes fastest.
Arguments:
- frames: float32 [16, 64, 64, 4096], P('ta', 'sa'), may hold values from -6 to 6
- taps: float32 [7], replicated, may hold values from 0.1 to 0.3
Outputs:
- columns: float32 [64, 16, 512, 512], P('sa', 'ta')
All inputs are finite; a program needn't handle non-finite values.
Results may differ from a plain program's by a relative error of at most 0.00002.
Values sent between devices are 32-bit elements; how exact they have to be, the bound alone decides.
A program may use at most 128 MiB of HBM per device.

v0:
```python
import jax
import jax.numpy as jnp
from jax import lax
from jax.sharding import PartitionSpec as P

TS = 512


def extended_2(cells, sides, width):
    for axis, dim in sides:
        count = lax.axis_size(axis)
        ends = count - 1
        head = lax.slice_in_dim(cells, 0, width, axis=dim)
        tail = lax.slice_in_dim(cells, cells.shape[dim] - width, cells.shape[dim], axis=dim)
        cells = jnp.concatenate(
            [
                lax.ppermute(tail, axis, [(i, (i + 1) % count) for i in range(ends)]),
                cells,
                lax.ppermute(head, axis, [((i + 1) % count, i) for i in range(ends)]),
            ],
            axis=dim,
        )
    return cells


def pack_tiles(block, readers):
    count = block.shape[0]
    per_tile = TS // readers
    tile_rows = block.shape[2] // per_tile
    tile_cols = block.shape[3] // TS
    shaped = block.reshape(count, tile_rows, per_tile, tile_cols, TS)
    return shaped.transpose(1, 3, 0, 2, 4).reshape(tile_rows * tile_cols, 1, count, per_tile, TS)


def unpack_tiles(received):
    owned = received.shape[0]
    count = received.shape[2]
    return received.transpose(0, 2, 3, 1, 4).reshape(owned, count, TS, TS)


def on_device(frames, taps):
    steps = frames.shape[0]
    readers = lax.axis_size("sa")
    received = lax.all_to_all(
        pack_tiles(frames, readers), "sa", split_axis=0, concat_axis=1, tiled=True
    )
    tiles = unpack_tiles(received)
    extended = extended_2(tiles, (("ta", 1),), 3)
    total = jnp.zeros((extended.shape[0], steps, TS, TS), jnp.float32)
    for offset in range(7):
        total = total + taps[offset] * extended[:, offset : offset + steps]
    return total


def solution(mesh):
    placed = (P("ta", "sa", None, None), P())
    return jax.shard_map(
        on_device, mesh=mesh, in_specs=placed, out_specs=P("sa", "ta", None, None), check_vma=False
    )
```

profile of v0, /device:TPU:64, one launch (start us, length us, event | category | flops | bytes accessed | tf_op | source)
XLA Modules:
  0.0 226.1 jit_solution(10796065754522443650)
XLA Ops:
  0.0 2.8 %copy.5 = f32[4,8,8,8,512]{4,2,0,3,1:T(8,128)S(1)} copy(f32[4,8,8,8,512]{4,2,3,1,0:T(8,128)} %bitcast.19) | data formatting | bytes 8388608 | tf_op jit(solution)/shard_map/reshape | solution.py:31
  2.8 60.1 %all_to_all.12 = f32[64,1,4,8,512]{4,3,2,1,0:T(8,128)S(1)} all-to-all(f32[64,1,4,8,512]{4,3,2,1,0:T(8,128)S(1)} %bitcast.18), channel_id=1, replica_groups=mesh['ta'=4,'sa'=64] {'sa'}, dimensions={0} | all-to-all | bytes 8388608 | tf_op jit(solution)/shard_map/all_to_all | solution.py:44
  63.0 2.4 %copy.6 = f32[64,1,4,8,512]{4,0,3,2,1:T(8,128)S(1)} copy(f32[64,1,4,8,512]{4,3,2,1,0:T(8,128)S(1)} %all_to_all.12) | data formatting | bytes 8388608 | tf_op jit(solution)/shard_map/all_to_all | solution.py:44
  65.4 0.0 copy-start.1
  65.4 0.8 fusion.16
  66.2 5.5 %collective-permute-start = (f32[1,3,512,512]{3,2,1,0:T(8,128)S(1)}, f32[1,3,512,512]{3,2,1,0:T(8,128)S(1)}, u32[]{:S(2)}, u32[]{:S(2)}) collective-permute-start(f32[1,3,512,512]{3,2,1,0:T(8,128)S(1)} %get-tuple-element.5), channel_id=1, source_target_pairs={{0,64},{64,128},{128,192},{1,65},{65,129},{129,193},{2,66},{66,130... | collective-permute-start | bytes 9437192 | tf_op jit(solution)/shard_map/ppermute | solution.py:17
  71.7 1.9 collective-permute-start.1
  73.6 0.0 copy-done.1
  73.6 0.7 fusion.17
  74.3 131.7 %collective-permute-done = f32[1,3,512,512]{3,2,1,0:T(8,128)S(1)} collective-permute-done((f32[1,3,512,512]{3,2,1,0:T(8,128)S(1)}, f32[1,3,512,512]{3,2,1,0:T(8,128)S(1)}, u32[]{:S(2)}, u32[]{:S(2)}) %collective-permute-start) | collective-permute-done | bytes 3145760 | tf_op jit(solution)/shard_map/ppermute | solution.py:17
  206.0 7.0 %collective-permute-done.1 = f32[1,3,512,512]{3,2,1,0:T(8,128)S(1)} collective-permute-done((f32[1,3,512,512]{3,2,1,0:T(8,128)S(1)}, f32[1,3,512,512]{3,2,1,0:T(8,128)S(1)}, u32[]{:S(2)}, u32[]{:S(2)}) %collective-permute-start.1) | collective-permute-done | bytes 3145760 | tf_op jit(solution)/shard_map/ppermute | solution.py:19
  213.0 0.0 copy-start
  213.0 1.7 copy-done
  214.7 11.4 %fusion.3 = f32[1,4,512,512]{3,2,1,0:T(8,128)} fusion(f32[1,4,512,512]{3,2,1,0:T(8,128)S(1)} %bitcast.17, f32[1,3,512,512]{3,2,1,0:T(8,128)} %copy-done, f32[1,3,512,512]{3,2,1,0:T(8,128)S(1)} %collective-permute-done, f32[]{:T(128)} %bitcast.14, f32[]{:T(128)} %bitcast.13, f32[]{:T(128)} %bitcast.12, f32[]{:T(128)} %bitcast.9, f32[]{:T(128)} %bitcast.8, ...), kind=kLoop, calls=%fused_computation.11 | loop fusion | flops 19922944 | bytes 14680092 | tf_op jit(solution)/shard_map/add | solution.py:51
Async XLA Ops:
  65.4 8.2 %copy-start.1 = (f32[7]{0:T(128)S(1)}, f32[7]{0:T(128)}, u32[]{:S(2)}) copy-start(f32[7]{0:T(128)} %param.3) | copy-start | bytes 88
  66.2 139.8 %collective-permute-start = (f32[1,3,512,512]{3,2,1,0:T(8,128)S(1)}, f32[1,3,512,512]{3,2,1,0:T(8,128)S(1)}, u32[]{:S(2)}, u32[]{:S(2)}) collective-permute-start(f32[1,3,512,512]{3,2,1,0:T(8,128)S(1)} %get-tuple-element.5), channel_id=1, source_target_pairs={{0,64},{64,128},{128,192},{1,65},{65,129},{129,193},{2,66},{66,130... | collective-permute-start | bytes 9437192 | tf_op jit(solution)/shard_map/ppermute | solution.py:17
  71.7 141.3 %collective-permute-start.1 = (f32[1,3,512,512]{3,2,1,0:T(8,128)S(1)}, f32[1,3,512,512]{3,2,1,0:T(8,128)S(1)}, u32[]{:S(2)}, u32[]{:S(2)}) collective-permute-start(f32[1,3,512,512]{3,2,1,0:T(8,128)S(1)} %get-tuple-element.6), channel_id=1, source_target_pairs={{64,0},{128,64},{192,128},{65,1},{129,65},{193,129},{66,2},{130,66... | collective-permute-start | bytes 9437192 | tf_op jit(solution)/shard_map/ppermute | solution.py:19
  213.0 1.7 copy-start
where the time goes:
time: 227 us; the launch traced here: 226 us
  waiting for transfers between devices  139 us (61%)
  blocking collectives  60.1 us (26%)
  other arithmetic  11.4 us (5%)
  local copies, waits for them, and re-layouts  8.37 us (4%)
  starting transfers between devices  7.41 us (3%)
    ppermute x1, waiting for transfers between devices, extended_2(): lax.ppermute(tail, axis, [(i, (i + 1) % count) for i in range(ends)])  132 us
    all_to_all x1, blocking collectives, on_device(): lax.all_to_all(pack_tiles(frames, readers), 'sa', split_axis=0, concat_ax...  60.1 us
    add x1, other arithmetic, on_device(): total = total + taps[offset] * extended[:, offset:offset + steps]  11.4 us
    ppermute x1, waiting for transfers between devices, extended_2(): lax.ppermute(head, axis, [((i + 1) % count, i) for i in range(ends)])  6.99 us
    ppermute x1, starting transfers between devices, extended_2(): lax.ppermute(tail, axis, [(i, (i + 1) % count) for i in range(ends)])  5.49 us
  transfers between devices with their start and end apart: 2, of which 2 were waited for; matrix products, arithmetic and copies ran while one was open for 0% of the time, Pallas kernels for 0%

commit v1 on v0

v1 whole, which is shorter than its diff:
```python
import functools

import jax
import jax.numpy as jnp
from jax import lax
from jax.experimental import pallas as pl
from jax.experimental.pallas import tpu as pltpu
from jax.sharding import PartitionSpec as P

TS = 512
NX = 4
NYC = 4
SLOTS = NX * NYC * 2
OFFSETS = (
    (0, 0), (1, 0), (0, 1), (3, 0), (0, 3), (1, 1), (3, 3), (1, 3),
    (3, 1), (2, 0), (0, 2), (2, 1), (1, 2), (2, 3), (3, 2), (2, 2),
)
LAG_HALO = 3
LAG_FWD = 8


def kernel(
    groups, taps_ref, frames, out, plane, cross, halo, total,
    own_sem, in_send, in_recv, x_send, x_recv, h_send, h_recv, out_sem,
):
    g = lax.axis_index("ta")
    s = lax.axis_index("sa")
    c = s % 2
    x = (s // 2) % NX
    a = (s // (2 * NX)) % 2
    y = s // (4 * NX)
    mine = (y * NX + x) * 2 + c
    last = groups - 1

    def device(group, yy, zz, xx, cc):
        return (group, ((yy * 2 + zz) * NX + xx) * 2 + cc)

    def chip(k, sign):
        dx, dy = OFFSETS[k]
        return (x + (dx if sign > 0 else NX - dx)) % NX, (y + (dy if sign > 0 else NYC - dy)) % NYC

    step = 2 * a - 1
    beyond = g + step
    has_up = g < last
    has_down = g > 0
    has_beyond = jnp.logical_and(beyond >= 0, beyond <= last)

    def piece(xx, yy, cc):
        return frames.at[:, pl.ds(2 * yy, 2), :, pl.ds(pl.multiple_of(TS * (2 * xx + cc), TS), TS)]

    own = pltpu.make_async_copy(piece(x, y, c), plane.at[mine], own_sem)
    own.start()

    barrier = pltpu.get_barrier_semaphore()

    def greet(target):
        pl.semaphore_signal(barrier, inc=1, device_id=target, device_id_type=pl.DeviceIdType.MESH)

    for k in range(len(OFFSETS)):
        xx, yy = chip(k, 1)
        for other in range(2):
            cc = (c + 1 - other) % 2
            if k == 0 and other == 1:
                continue
            greet(device(g, yy, a, xx, cc))
    greet(device(g, y, 1 - a, x, c))

    @pl.when(has_up)
    def _():
        greet(device(g + 1, y, a, x, c))

    @pl.when(has_down)
    def _():
        greet(device(g - 1, y, a, x, c))

    @pl.when(has_beyond)
    def _():
        greet(device(beyond, y, 1 - a, x, c))

    count = (
        2 * len(OFFSETS) - 1 + 1 + has_up.astype(jnp.int32)
        + has_down.astype(jnp.int32) + has_beyond.astype(jnp.int32)
    )
    pl.semaphore_wait(barrier, count)

    def in_plane(k, other):
        xx, yy = chip(k, 1)
        cc = (c + 1 - other) % 2
        return pltpu.make_async_remote_copy(
            src_ref=piece(xx, yy, cc), dst_ref=plane.at[mine],
            send_sem=in_send.at[2 * k + other], recv_sem=in_recv.at[mine],
            device_id=device(g, yy, a, xx, cc), device_id_type=pl.DeviceIdType.MESH,
        )

    def arrival(slot):
        return pltpu.make_async_remote_copy(
            src_ref=piece(x, y, c), dst_ref=plane.at[slot],
            send_sem=in_send.at[0], recv_sem=in_recv.at[slot],
            device_id=device(g, y, 1 - a, x, c), device_id_type=pl.DeviceIdType.MESH,
        )

    for k in range(len(OFFSETS)):
        for other in range(2):
            if k == 0 and other == 1:
                continue
            in_plane(k, other).start()

    def zero(side):
        def body(i, _):
            halo[side, i // SLOTS, i % SLOTS] = jnp.zeros((3, 8, TS), jnp.float32)
            return 0
        lax.fori_loop(0, 2 * SLOTS, body, 0)

    @pl.when(jnp.logical_not(has_down))
    def _():
        zero(0)

    @pl.when(jnp.logical_not(has_up))
    def _():
        zero(1)

    def chip_of(k):
        xx, yy = chip(k, -1)
        return yy * NX + xx

    def cross_copy(k):
        m = chip_of(k)
        return pltpu.make_async_remote_copy(
            src_ref=plane.at[pl.ds(2 * m, 2), :, 1 - a], dst_ref=cross.at[pl.ds(2 * m, 2)],
            send_sem=x_send.at[m], recv_sem=x_recv.at[m],
            device_id=device(g, y, 1 - a, x, c), device_id_type=pl.DeviceIdType.MESH,
        )

    def halo_copy(k, src, start, side, rel, target):
        m = chip_of(k)
        return pltpu.make_async_remote_copy(
            src_ref=src, dst_ref=halo.at[side, rel, pl.ds(2 * m, 2)],
            send_sem=h_send.at[side, rel, m], recv_sem=h_recv.at[side, rel, m],
            device_id=target, device_id_type=pl.DeviceIdType.MESH,
        )

    def up(k):
        m = chip_of(k)
        return halo_copy(k, plane.at[pl.ds(2 * m, 2), pl.ds(1, 3), a], 1, 0, 0, device(g + 1, y, a, x, c))

    def down(k):
        m = chip_of(k)
        return halo_copy(k, plane.at[pl.ds(2 * m, 2), pl.ds(0, 3), a], 0, 1, 0, device(g - 1, y, a, x, c))

    def side_copy(k):
        m = chip_of(k)
        return pltpu.make_async_remote_copy(
            src_ref=plane.at[pl.ds(2 * m, 2), pl.ds(a, 3), 1 - a],
            dst_ref=halo.at[1 - a, 1, pl.ds(2 * m, 2)],
            send_sem=h_send.at[a, 1, m], recv_sem=h_recv.at[1 - a, 1, m],
            device_id=device(beyond, y, 1 - a, x, c), device_id_type=pl.DeviceIdType.MESH,
        )

    def forward(k):
        m = chip_of(k)
        return pltpu.make_async_remote_copy(
            src_ref=cross.at[pl.ds(2 * m, 2), pl.ds(a, 3)],
            dst_ref=halo.at[1 - a, 1, pl.ds(2 * m, 2)],
            send_sem=h_send.at[1 - a, 1, m], recv_sem=h_recv.at[1 - a, 1, m],
            device_id=device(beyond, y, a, x, c), device_id_type=pl.DeviceIdType.MESH,
        )

    def start_if(flag, make):
        @pl.when(flag)
        def _():
            make().start()

    n = len(OFFSETS)
    for k in range(n + max(LAG_HALO, LAG_FWD)):
        if k < n:
            m = chip_of(k)
            if k == 0:
                own.wait()
                arrival(2 * m + 1 - c).wait_recv()
            else:
                arrival(2 * m).wait_recv()
                arrival(2 * m + 1).wait_recv()
            cross_copy(k).start()
            start_if(has_beyond, lambda: side_copy(k))
        if 0 <= k - LAG_HALO < n:
            start_if(has_up, lambda: up(k - LAG_HALO))
            start_if(has_down, lambda: down(k - LAG_HALO))
        if 0 <= k - LAG_FWD < n:
            cross_copy(k - LAG_FWD).wait_recv()
            start_if(has_beyond, lambda: forward(k - LAG_FWD))

    taps = [taps_ref[j] for j in range(7)]

    def out_copy(k, rel):
        m = chip_of(k)
        z = a if rel == 0 else 1 - a
        row = (m // NX) * 4 * NX + z * 2 * NX + (m % NX) * 2
        return pltpu.make_async_copy(
            total.at[:, pl.ds(row, 2)], out.at[:, pl.ds(row, 2)], out_sem.at[rel, m]
        )

    def sum_rows(k, rel):
        m = chip_of(k)
        z = a if rel == 0 else 1 - a
        row = (m // NX) * 4 * NX + z * 2 * NX + (m % NX) * 2
        for i in range(2):
            slot = 2 * m + i
            values = [halo[0, rel, slot, j] for j in range(3)]
            if rel == 0:
                values += [plane[slot, j, a] for j in range(4)]
            else:
                values += [cross[slot, j] for j in range(4)]
            values += [halo[1, rel, slot, j] for j in range(3)]
            for t in range(4):
                acc = taps[0] * values[t]
                for j in range(1, 7):
                    acc = acc + taps[j] * values[t + j]
                total[t, row + i] = acc

    for rel in range(2):
        for k in range(n):
            m = chip_of(k)
            for side, flag in ((0, has_down), (1, has_up)):
                @pl.when(flag)
                def _():
                    halo_copy(
                        k, plane.at[pl.ds(2 * m, 2), pl.ds(0, 3), a], 0, side, rel,
                        device(g, y, 1 - a, x, c),
                    ).wait_recv()
            sum_rows(k, rel)
            out_copy(k, rel).start()

    for k in range(n):
        for other in range(2):
            if k == 0 and other == 1:
                continue
            in_plane(k, other).wait_send()
        cross_copy(k).wait_send()

        @pl.when(has_up)
        def _():
            up(k).wait_send()

        @pl.when(has_down)
        def _():
            down(k).wait_send()

        @pl.when(has_beyond)
        def _():
            side_copy(k).wait_send()
            forward(k).wait_send()
        out_copy(k, 0).wait()
        out_copy(k, 1).wait()


def on_device(groups, frames, taps):
    shaped = frames.reshape(4, 8, 8, frames.shape[3])
    chips = NX * NYC
    summed = pl.pallas_call(
        functools.partial(kernel, groups),
        out_shape=jax.ShapeDtypeStruct((4, 2 * SLOTS, 8, TS), jnp.float32),
        in_specs=[pl.BlockSpec(memory_space=pltpu.SMEM), pl.BlockSpec(memory_space=pl.ANY)],
        out_specs=pl.BlockSpec(memory_space=pl.ANY),
        scratch_shapes=[
            pltpu.VMEM((SLOTS, 4, 2, 8, TS), jnp.float32),
            pltpu.VMEM((SLOTS, 4, 8, TS), jnp.float32),
            pltpu.VMEM((2, 2, SLOTS, 3, 8, TS), jnp.float32),
            pltpu.VMEM((4, 2 * SLOTS, 8, TS), jnp.float32),
            pltpu.SemaphoreType.DMA,
            pltpu.SemaphoreType.DMA((SLOTS,)),
            pltpu.SemaphoreType.DMA((SLOTS,)),
            pltpu.SemaphoreType.DMA((chips,)),
            pltpu.SemaphoreType.DMA((chips,)),
            pltpu.SemaphoreType.DMA((2, 2, chips)),
            pltpu.SemaphoreType.DMA((2, 2, chips)),
            pltpu.SemaphoreType.DMA((2, chips)),
        ],
        compiler_params=pltpu.CompilerParams(collective_id=0, has_side_effects=True),
        name="exchange",
    )(taps, shaped)
    return summed.transpose(0, 2, 1, 3).reshape(1, 4, TS, TS)


def solution(mesh):
    placed = (P("ta", "sa", None, None), P())
    return jax.shard_map(
        functools.partial(on_device, mesh.shape["ta"]),
        mesh=mesh, in_specs=placed, out_specs=P("sa", "ta", None, None), check_vma=False,
    )
```

time: 227 us -> 174 us (0.77)
  Pallas kernels: 0 us -> 167 us
  waiting for transfers between devices: 139 us -> 0 us
  blocking collectives: 60.1 us -> 0 us
  other arithmetic: 11.4 us -> 0 us
  starting transfers between devices: 7.41 us -> 0 us
    pallas_call x0 -> x1, Pallas kernels: none -> 167 us  [on_device(): pl.pallas_call(functools.partial(kernel, groups), out_shape=jax.ShapeDtyp...]
    ppermute x2 -> x0, waiting for transfers between devices: 139 us -> none  [the longest x1 132 us: extended_2(): lax.ppermute(tail, axis, [(i, (i + 1) % count) for i in range(ends)])]
    all_to_all x1 -> x0, blocking collectives: 60.1 us -> none  [on_device(): lax.all_to_all(pack_tiles(frames, readers), 'sa', split_axis=0, concat_ax...]
    add x1 -> x0, other arithmetic: 11.4 us -> none  [on_device(): total = total + taps[offset] * extended[:, offset:offset + steps]]
    ppermute x2 -> x0, starting transfers between devices: 7.41 us -> none  [the longest x1 5.49 us: extended_2(): lax.ppermute(tail, axis, [(i, (i + 1) % count) for i in range(ends)])]
    transpose x0 -> x1, local copies, waits for them, and re-layouts: none -> 6.63 us  [on_device(): return summed.transpose(0, 2, 1, 3).reshape(1, 4, TS, TS)]
    reshape x1 -> x0, local copies, waits for them, and re-layouts: 2.83 us -> none  [pack_tiles(): shaped = block.reshape(count, tile_rows, per_tile, tile_cols, TS)]
    all_to_all x1 -> x0, local copies, waits for them, and re-layouts: 2.43 us -> none  [on_device(): lax.all_to_all(pack_tiles(frames, readers), 'sa', split_axis=0, concat_ax...]
  transfers between devices with their start and end apart: 2 -> 0, of which waited for: 2 -> 0; matrix products, arithmetic and copies ran while one was open for 0% -> 0% of each run, Pallas kernels for 0% -> 0%
where the time goes in v1:
time: 174 us
  Pallas kernels  167 us (96%)
  local copies, waits for them, and re-layouts  6.63 us (4%)
    pallas_call x1, Pallas kernels, on_device(): pl.pallas_call(functools.partial(kernel, groups), out_shape=jax.ShapeDtyp...  167 us
    transpose x1, local copies, waits for them, and re-layouts, on_device(): return summed.transpose(0, 2, 1, 3).reshape(1, 4, TS, TS)  6.63 us

profile of v1, /device:TPU:64, one launch (start us, length us, event | category | flops | bytes accessed | tf_op | source)
XLA Modules:
  0.0 173.8 jit_solution(14538590045605495972)
XLA Ops:
  0.0 167.2 %exchange.1 = f32[4,64,8,512]{3,2,1,0:T(8,128)} custom-call(f32[7]{0:T(128)} %taps_ref.1, f32[4,8,8,4096]{3,2,1,0:T(8,128)} %bitcast.4), custom_call_target="tpu_custom_call" | custom-call | tf_op jit(solution)/shard_map/exchange/pallas_call | solution.py:259
  167.2 6.6 %copy.3 = f32[4,8,64,512]{3,2,1,0:T(8,128)} copy(f32[4,8,64,512]{3,1,2,0:T(8,128)} %bitcast.3) | data formatting | bytes 8388608 | tf_op jit(solution)/shard_map/transpose | solution.py:281

commit v2 on v0

v2 whole, which is shorter than its diff:
```python
import functools

import jax
import jax.numpy as jnp
from jax import lax
from jax.experimental import pallas as pl
from jax.experimental.pallas import tpu as pltpu
from jax.sharding import PartitionSpec as P

TS = 512
NX = 4
CHIPS = NX * NX
SLOTS = 2 * CHIPS
MESH = pl.DeviceIdType.MESH

UNITS = (
    ('one', 0, 0),
    ('one', 0, 1),
    ('one', 1, 0),
    ('one', 4, 0),
    ('one', 3, 0),
    ('one', 12, 0),
    ('one', 1, 1),
    ('one', 4, 1),
    ('one', 3, 1),
    ('one', 12, 1),
    ('chip', 5),
    ('chip', 13),
    ('chip', 2),
    ('pair', 8),
    ('pair', 6),
    ('pair', 14),
    ('pair', 10),
)
SENDS = (
    (0, 1),
    (1, 0),
    (4, 0),
    (3, 0),
    (12, 0),
    (1, 1),
    (4, 1),
    (3, 1),
    (12, 1),
    (5, 0),
    (5, 1),
    (13, 0),
    (13, 1),
    (2, 0),
    (2, 1),
    (8, 0),
    (8, 1),
    (9, 0),
    (9, 1),
    (6, 0),
    (6, 1),
    (7, 0),
    (7, 1),
    (14, 0),
    (14, 1),
    (15, 0),
    (15, 1),
    (10, 0),
    (10, 1),
    (11, 0),
    (11, 1),
)
SIZES = {"one": 1, "chip": 2, "pair": 4}
STEPS = len(UNITS)
LAGS = dict(P=0, S1=0, Nf=0, N=0, F=3, R1=4, R3=2, X=37, W=37, A=31, R2=39, B=65)
ORDER = tuple(
    (kind, step - lag)
    for step in range(STEPS + max(LAGS.values()))
    for kind, lag in LAGS.items()
    if 0 <= step - lag < STEPS
)


def unit_of(offset, other):
    for u, unit in enumerate(UNITS):
        if unit[0] == "one":
            hit = unit[1:] == (offset, other)
        elif unit[0] == "chip":
            hit = unit[1] == offset
        else:
            hit = unit[1] // 2 == offset // 2
        if hit:
            return u


def flipped(v, bits):
    return (v, v + 1 - 2 * (v % 2), (v + 2) % NX, NX - 1 - v)[bits]


def kernel(
    groups, taps_hbm, frames, out, taps_ref, plane, cross, relay, halo,
    taps_sem, own_sem, in_send, in_recv, x_recv, z_send, r_recv, h_recv,
):
    g = lax.axis_index("ta")
    s = lax.axis_index("sa")
    c = s % 2
    x = (s // 2) % NX
    a = (s // (2 * NX)) % 2
    y = s // (4 * NX)
    mine = (y * NX + x) * 2 + c
    last = groups - 1
    step = 2 * a - 1
    beyond, near = g + step, g - step
    has_near = jnp.logical_and(near >= 0, near <= last)
    has_far = jnp.logical_and(beyond >= 0, beyond <= last)
    has_up = g < last
    has_down = g > 0

    def device(group, yy, zz, xx, cc):
        return (group, ((yy * 2 + zz) * NX + xx) * 2 + cc)

    def chip(offset):
        return flipped(y, offset // NX), flipped(x, offset % NX)

    partner = device(g, y, 1 - a, x, c)
    beyond_chip = device(beyond, y, 1 - a, x, c)

    def slots(u):
        unit = UNITS[u]
        yy, xx = chip(unit[1])
        base = 2 * (yy * NX + xx)
        if unit[0] == "one":
            return pl.ds(base + (c if unit[2] == 0 else 1 - c), 1)
        if unit[0] == "pair":
            base = base // 4 * 4
        return pl.ds(base, SIZES[unit[0]])

    def piece(yy, xx, cc):
        return frames.at[:, pl.ds(2 * yy, 2), :, pl.ds(pl.multiple_of(TS * (2 * xx + cc), TS), TS)]

    own = pltpu.make_async_copy(piece(y, x, c), plane.at[mine], own_sem)
    own.start()
    weights = pltpu.make_async_copy(taps_hbm, taps_ref, taps_sem)
    weights.start()

    barrier = pltpu.get_barrier_semaphore()

    def greet(target):
        pl.semaphore_signal(barrier, inc=1, device_id=target, device_id_type=MESH)

    for offset, other in reversed(SENDS):
        yy, xx = chip(offset)
        greet(device(g, yy, a, xx, (c + other) % 2))
    greet(partner)

    @pl.when(has_far)
    def _():
        greet(beyond_chip)

    pl.semaphore_wait(barrier, SLOTS + has_far.astype(jnp.int32))

    def remote(src, dst, send, recv, target):
        return pltpu.make_async_remote_copy(
            src_ref=src, dst_ref=dst, send_sem=send, recv_sem=recv,
            device_id=target, device_id_type=MESH,
        )

    def in_plane(offset, other):
        yy, xx = chip(offset)
        cc = (c + other) % 2
        return remote(
            piece(yy, xx, cc), plane.at[mine], in_send, in_recv.at[unit_of(offset, other)],
            device(g, yy, a, xx, cc),
        )

    def cross_copy(u):
        return remote(
            plane.at[slots(u), :, 1 - a], cross.at[slots(u)], z_send.at[7], x_recv.at[u], partner
        )

    def near_halo(u):
        return remote(
            plane.at[slots(u), pl.ds(1 - a, 3), a], relay.at[0, slots(u)],
            z_send.at[0], r_recv.at[0, u], partner,
        )

    def far_halo(u):
        return remote(
            plane.at[slots(u), pl.ds(a, 3), a], relay.at[1, slots(u)],
            z_send.at[1], r_recv.at[1, u], beyond_chip,
        )

    def side_halo(u):
        return remote(
            plane.at[slots(u), pl.ds(a, 3), 1 - a], halo.at[1 - a, 1, slots(u)],
            z_send.at[2], h_recv.at[1 - a, 1, u], beyond_chip,
        )

    def forward(u):
        return remote(
            cross.at[slots(u), pl.ds(a, 3)], relay.at[2, slots(u)],
            z_send.at[3], r_recv.at[2, u], beyond_chip,
        )

    def relay_near(u, w):
        return remote(
            relay.at[1 + w, slots(u)], halo.at[a, w, slots(u)],
            z_send.at[4 + w], h_recv.at[a, w, u], partner,
        )

    def relay_far(u):
        return remote(
            relay.at[0, slots(u)], halo.at[1 - a, 0, slots(u)],
            z_send.at[6], h_recv.at[1 - a, 0, u], beyond_chip,
        )

    def wait_in(ref, sem):
        remote(ref, ref, in_send, sem, partner).wait_recv()

    def wait_out(ref, sem):
        remote(ref, ref, sem, own_sem, partner).wait_send()


    for offset, other in SENDS:
        in_plane(offset, other).start()

    def zero(side):
        def body(i, _):
            halo[side, i // SLOTS, i % SLOTS] = jnp.zeros((3, 8, TS), jnp.float32)
            return 0
        lax.fori_loop(0, 2 * SLOTS, body, 0)

    @pl.when(jnp.logical_not(has_down))
    def _():
        zero(0)

    @pl.when(jnp.logical_not(has_up))
    def _():
        zero(1)

    weights.wait()
    taps = [taps_ref[j] for j in range(7)]

    def sum_rows(u, rel):
        run = slots(u)

        def body(i, _):
            slot = run.start + i
            m = slot // 2
            z = a if rel == 0 else 1 - a
            row = ((m // NX) * 2 + z) * 32 + (m % NX) * 2 + slot % 2
            for q in range(TS // 128):
                lanes = pl.ds(q * 128, 128)
                values = [halo[0, rel, slot, j, :, lanes] for j in range(3)]
                if rel == 0:
                    values += [plane[slot, j, a, :, lanes] for j in range(4)]
                else:
                    values += [cross[slot, j, :, lanes] for j in range(4)]
                values += [halo[1, rel, slot, j, :, lanes] for j in range(3)]
                for t in range(4):
                    acc = taps[0] * values[t]
                    for j in range(1, 7):
                        acc = acc + taps[j] * values[t + j]
                    out[t, pl.ds(row + 8 * q, 8, stride=TS // 8 * 4), :] = acc
            return 0

        lax.fori_loop(0, run.size, body, 0)

    def finish(u, rel):
        for side, flag in ((0, has_down), (1, has_up)):
            @pl.when(flag)
            def _():
                wait_in(halo.at[side, rel, slots(u)], h_recv.at[side, rel, u])
        sum_rows(u, rel)

    for kind, u in ORDER:
        if kind == "P":
            if u == 0:
                own.wait()
            else:
                wait_in(plane.at[slots(u)], in_recv.at[u])
        elif kind == "S1":
            cross_copy(u).start()
        elif kind == "N":
            @pl.when(has_near)
            def _():
                near_halo(u).start()
        elif kind == "A":
            finish(u, 0)
        elif kind == "X":
            wait_in(cross.at[slots(u)], x_recv.at[u])
        elif kind == "B":
            finish(u, 1)
        else:
            @pl.when(has_far)
            def _():
                if kind == "Nf":
                    far_halo(u).start()
                elif kind == "F":
                    side_halo(u).start()
                elif kind == "W":
                    forward(u).start()
                elif kind == "R1":
                    wait_in(relay.at[1, slots(u)], r_recv.at[1, u])
                    relay_near(u, 0).start()
                elif kind == "R2":
                    wait_in(relay.at[2, slots(u)], r_recv.at[2, u])
                    relay_near(u, 1).start()
                elif kind == "R3":
                    wait_in(relay.at[0, slots(u)], r_recv.at[0, u])
                    relay_far(u).start()

    wait_out(plane.at[pl.ds(0, SLOTS - 1)], in_send)
    wait_out(cross, z_send.at[7])

    @pl.when(has_near)
    def _():
        wait_out(relay.at[0], z_send.at[0])

    @pl.when(has_far)
    def _():
        for kind in range(1, 7):
            wait_out(relay.at[0], z_send.at[kind])


def on_device(groups, frames, taps):
    shaped = frames.reshape(4, 8, 8, frames.shape[3])
    summed = pl.pallas_call(
        functools.partial(kernel, groups),
        out_shape=jax.ShapeDtypeStruct((4, 4 * TS, 128), jnp.float32),
        in_specs=[pl.BlockSpec(memory_space=pltpu.HBM), pl.BlockSpec(memory_space=pltpu.HBM)],
        out_specs=pl.BlockSpec(memory_space=pltpu.VMEM),
        scratch_shapes=[
            pltpu.SMEM((7,), jnp.float32),
            pltpu.VMEM((SLOTS, 4, 2, 8, TS), jnp.float32),
            pltpu.VMEM((SLOTS, 4, 8, TS), jnp.float32),
            pltpu.VMEM((3, SLOTS, 3, 8, TS), jnp.float32),
            pltpu.VMEM((2, 2, SLOTS, 3, 8, TS), jnp.float32),
            pltpu.SemaphoreType.DMA,
            pltpu.SemaphoreType.DMA,
            pltpu.SemaphoreType.DMA,
            pltpu.SemaphoreType.DMA((STEPS,)),
            pltpu.SemaphoreType.DMA((STEPS,)),
            pltpu.SemaphoreType.DMA((8,)),
            pltpu.SemaphoreType.DMA((3, STEPS)),
            pltpu.SemaphoreType.DMA((2, 2, STEPS)),
        ],
        compiler_params=pltpu.CompilerParams(
            collective_id=0, has_side_effects=True, vmem_limit_bytes=24 * 2**20
        ),
        name="exchange",
    )(
        pltpu.with_memory_space_constraint(taps, pltpu.HBM),
        pltpu.with_memory_space_constraint(shaped, pltpu.HBM),
    )
    tiled = summed.reshape(4, TS // 8, TS // 128, 8, 128)
    return tiled.transpose(0, 1, 3, 2, 4).reshape(1, 4, TS, TS)


def solution(mesh):
    placed = (P("ta", "sa", None, None), P())
    return jax.shard_map(
        functools.partial(on_device, mesh.shape["ta"]),
        mesh=mesh, in_specs=placed, out_specs=P("sa", "ta", None, None), check_vma=False,
    )
```

time: 227 us -> 164 us (0.72)
  Pallas kernels: 0 us -> 159 us
  waiting for transfers between devices: 139 us -> 0 us
  blocking collectives: 60.1 us -> 0 us
  other arithmetic: 11.4 us -> 0 us
  starting transfers between devices: 7.41 us -> 0 us
  local copies, waits for them, and re-layouts: 8.37 us -> 2.02 us
    pallas_call x0 -> x1, Pallas kernels: none -> 159 us  [on_device(): pl.pallas_call(functools.partial(kernel, groups), out_shape=jax.ShapeDtyp...]
    ppermute x2 -> x0, waiting for transfers between devices: 139 us -> none  [the longest x1 132 us: extended_2(): lax.ppermute(tail, axis, [(i, (i + 1) % count) for i in range(ends)])]
    all_to_all x1 -> x0, blocking collectives: 60.1 us -> none  [on_device(): lax.all_to_all(pack_tiles(frames, readers), 'sa', split_axis=0, concat_ax...]
    add x1 -> x0, other arithmetic: 11.4 us -> none  [on_device(): total = total + taps[offset] * extended[:, offset:offset + steps]]
    ppermute x2 -> x0, starting transfers between devices: 7.41 us -> none  [the longest x1 5.49 us: extended_2(): lax.ppermute(tail, axis, [(i, (i + 1) % count) for i in range(ends)])]
    reshape x1 -> x0, local copies, waits for them, and re-layouts: 2.83 us -> none  [pack_tiles(): shaped = block.reshape(count, tile_rows, per_tile, tile_cols, TS)]
    all_to_all x1 -> x0, local copies, waits for them, and re-layouts: 2.43 us -> none  [on_device(): lax.all_to_all(pack_tiles(frames, readers), 'sa', split_axis=0, concat_ax...]
  transfers between devices with their start and end apart: 2 -> 0, of which waited for: 2 -> 0; matrix products, arithmetic and copies ran while one was open for 0% -> 0% of each run, Pallas kernels for 0% -> 0%
where the time goes in v2:
time: 164 us; the launch traced here: 161 us
  Pallas kernels  159 us (97%)
  local copies, waits for them, and re-layouts  2.02 us (1%)
    pallas_call x1, Pallas kernels, on_device(): pl.pallas_call(functools.partial(kernel, groups), out_shape=jax.ShapeDtyp...  159 us

profile of v2, /device:TPU:64, one launch (start us, length us, event | category | flops | bytes accessed | tf_op | source)
XLA Modules:
  0.0 160.8 jit_solution(1640620884403906509)
XLA Ops:
  0.0 158.8 %exchange.1 = f32[4,2048,128]{2,1,0:T(8,128)S(1)} custom-call(f32[7]{0:T(128)} %taps_hbm.1, f32[4,8,8,4096]{3,2,1,0:T(8,128)} %bitcast.7), custom_call_target="tpu_custom_call" | custom-call | tf_op jit(solution)/shard_map/exchange/pallas_call | solution.py:323
  158.8 2.0 %copy.4 = f32[1,4,512,512]{3,2,1,0:T(8,128)} copy(f32[1,4,512,512]{3,2,1,0:T(8,128)S(1)} %bitcast.6) | data formatting | bytes 8388608

commit v3 on v2

--- a/solution.py
+++ b/solution.py
@@ -65,14 +65,18 @@
     (11, 0),
     (11, 1),
 )
+CLOSE = tuple(t for t in SENDS if t[0] // 4 == 0 or t[0] % 4 == 0)
 SIZES = {"one": 1, "chip": 2, "pair": 4}
 STEPS = len(UNITS)
-LAGS = dict(P=0, S1=0, Nf=0, N=0, F=3, R1=4, R3=2, X=37, W=37, A=31, R2=39, B=65)
+GROUPS = (tuple(range(2, 10)), (0, 1, 10, 11), (12, 13), (14,), (15,), (16,))
+GROUP_OF = {u: i for i, units in enumerate(GROUPS) for u in units}
+LAGS = dict(P=0, S1=0, Nf=0, N=0, F=0, R1=1, R3=35, X=4, W=4, R2=14, A=50, B=58)
 ORDER = tuple(
     (kind, step - lag)
     for step in range(STEPS + max(LAGS.values()))
     for kind, lag in LAGS.items()
-    if 0 <= step - lag < STEPS
+    if 0 <= step - lag < (len(GROUPS) if kind in "AB" else STEPS)
+    and (step > lag or kind not in ("P", "S1", "N", "Nf", "F"))
 )
 
 
@@ -94,7 +98,7 @@
 
 def kernel(
     groups, taps_hbm, frames, out, taps_ref, plane, cross, relay, halo,
-    taps_sem, own_sem, in_send, in_recv, x_recv, z_send, r_recv, h_recv,
+    taps_sem, own_sem, row_sem, in_send, in_recv, x_recv, z_send, r_recv, h_recv,
 ):
     g = lax.axis_index("ta")
     s = lax.axis_index("sa")
@@ -140,19 +144,19 @@
 
     barrier = pltpu.get_barrier_semaphore()
 
-    def greet(target):
-        pl.semaphore_signal(barrier, inc=1, device_id=target, device_id_type=MESH)
-
-    for offset, other in reversed(SENDS):
+    def signal(semaphore, target):
+        pl.semaphore_signal(semaphore, inc=1, device_id=target, device_id_type=MESH)
+
+    for offset, other in reversed(CLOSE):
         yy, xx = chip(offset)
-        greet(device(g, yy, a, xx, (c + other) % 2))
-    greet(partner)
+        signal(barrier, device(g, yy, a, xx, (c + other) % 2))
+    signal(barrier, partner)
 
     @pl.when(has_far)
     def _():
-        greet(beyond_chip)
-
-    pl.semaphore_wait(barrier, SLOTS + has_far.astype(jnp.int32))
+        signal(barrier, beyond_chip)
+
+    pl.semaphore_wait(barrier, len(CLOSE) + 1 + has_far.astype(jnp.int32))
 
     def remote(src, dst, send, recv, target):
         return pltpu.make_async_remote_copy(
@@ -188,7 +192,7 @@
     def side_halo(u):
         return remote(
             plane.at[slots(u), pl.ds(a, 3), 1 - a], halo.at[1 - a, 1, slots(u)],
-            z_send.at[2], h_recv.at[1 - a, 1, u], beyond_chip,
+            z_send.at[2], h_recv.at[1 - a, 1, GROUP_OF[u]], beyond_chip,
         )
 
     def forward(u):
@@ -200,13 +204,13 @@
     def relay_near(u, w):
         return remote(
             relay.at[1 + w, slots(u)], halo.at[a, w, slots(u)],
-            z_send.at[4 + w], h_recv.at[a, w, u], partner,
+            z_send.at[4 + w], h_recv.at[a, w, GROUP_OF[u]], partner,
         )
 
     def relay_far(u):
         return remote(
             relay.at[0, slots(u)], halo.at[1 - a, 0, slots(u)],
-            z_send.at[6], h_recv.at[1 - a, 0, u], beyond_chip,
+            z_send.at[6], h_recv.at[1 - a, 0, GROUP_OF[u]], beyond_chip,
         )
 
     def wait_in(ref, sem):
@@ -216,8 +220,27 @@
         remote(ref, ref, sem, own_sem, partner).wait_send()
 
 
+    for offset, other in CLOSE:
+        in_plane(offset, other).start()
+    for bits in range(1, NX):
+        signal(row_sem, device(g, y, a, flipped(x, bits), c))
+
+    own.wait()
+    cross_copy(0).start()
+
+    @pl.when(has_near)
+    def _():
+        near_halo(0).start()
+
+    @pl.when(has_far)
+    def _():
+        far_halo(0).start()
+        side_halo(0).start()
+
+    pl.semaphore_wait(row_sem, NX - 1)
     for offset, other in SENDS:
-        in_plane(offset, other).start()
+        if (offset, other) not in CLOSE:
+            in_plane(offset, other).start()
 
     def zero(side):
         def body(i, _):
@@ -261,19 +284,18 @@
 
         lax.fori_loop(0, run.size, body, 0)
 
-    def finish(u, rel):
+    def finish(group, rel):
+        readers = sum(SIZES[UNITS[u][0]] for u in GROUPS[group])
         for side, flag in ((0, has_down), (1, has_up)):
             @pl.when(flag)
             def _():
-                wait_in(halo.at[side, rel, slots(u)], h_recv.at[side, rel, u])
-        sum_rows(u, rel)
+                wait_in(halo.at[side, rel, pl.ds(0, readers)], h_recv.at[side, rel, group])
+        for u in GROUPS[group]:
+            sum_rows(u, rel)
 
     for kind, u in ORDER:
         if kind == "P":
-            if u == 0:
-                own.wait()
-            else:
-                wait_in(plane.at[slots(u)], in_recv.at[u])
+            wait_in(plane.at[slots(u)], in_recv.at[u])
         elif kind == "S1":
             cross_copy(u).start()
         elif kind == "N":
@@ -333,12 +355,13 @@
             pltpu.VMEM((2, 2, SLOTS, 3, 8, TS), jnp.float32),
             pltpu.SemaphoreType.DMA,
             pltpu.SemaphoreType.DMA,
+            pltpu.SemaphoreType.REGULAR,
             pltpu.SemaphoreType.DMA,
             pltpu.SemaphoreType.DMA((STEPS,)),
             pltpu.SemaphoreType.DMA((STEPS,)),
             pltpu.SemaphoreType.DMA((8,)),
             pltpu.SemaphoreType.DMA((3, STEPS)),
-            pltpu.SemaphoreType.DMA((2, 2, STEPS)),
+            pltpu.SemaphoreType.DMA((2, 2, len(GROUPS))),
         ],
         compiler_params=pltpu.CompilerParams(
             collective_id=0, has_side_effects=True, vmem_limit_bytes=24 * 2**20

time: 164 us -> 156 us (0.951); the launches traced: 161 us -> 156 us
  Pallas kernels: 159 us -> 154 us
    pallas_call x1, Pallas kernels: 159 us -> 154 us  [on_device(): pl.pallas_call(functools.partial(kernel, groups), out_shape=jax.ShapeDtyp...]
where the time goes in v3:
time: 156 us
  Pallas kernels  154 us (99%)
  local copies, waits for them, and re-layouts  2.02 us (1%)
    pallas_call x1, Pallas kernels, on_device(): pl.pallas_call(functools.partial(kernel, groups), out_shape=jax.ShapeDtyp...  154 us

profile of v3, /device:TPU:64, one launch (start us, length us, event | category | flops | bytes accessed | tf_op | source)
XLA Modules:
  0.0 155.9 jit_solution(12498639878311240057)
XLA Ops:
  0.0 153.9 %exchange.1 = f32[4,2048,128]{2,1,0:T(8,128)S(1)} custom-call(f32[7]{0:T(128)} %taps_hbm.1, f32[4,8,8,4096]{3,2,1,0:T(8,128)} %bitcast.7), custom_call_target="tpu_custom_call" | custom-call | tf_op jit(solution)/shard_map/exchange/pallas_call | solution.py:345
  153.9 2.0 %copy.4 = f32[1,4,512,512]{3,2,1,0:T(8,128)} copy(f32[1,4,512,512]{3,2,1,0:T(8,128)S(1)} %bitcast.6) | data formatting | bytes 8388608

commit v4 on v3

--- a/solution.py
+++ b/solution.py
@@ -22,11 +22,11 @@
     ('one', 12, 0),
     ('one', 1, 1),
     ('one', 4, 1),
+    ('one', 12, 1),
     ('one', 3, 1),
-    ('one', 12, 1),
+    ('chip', 2),
     ('chip', 5),
     ('chip', 13),
-    ('chip', 2),
     ('pair', 8),
     ('pair', 6),
     ('pair', 14),
@@ -69,13 +69,16 @@
 SIZES = {"one": 1, "chip": 2, "pair": 4}
 STEPS = len(UNITS)
 GROUPS = (tuple(range(2, 10)), (0, 1, 10, 11), (12, 13), (14,), (15,), (16,))
+ROUND = (13,)
+ROUND_SIZE = sum(SIZES[UNITS[u][0]] for u in ROUND)
 GROUP_OF = {u: i for i, units in enumerate(GROUPS) for u in units}
-LAGS = dict(P=0, S1=0, Nf=0, N=0, F=0, R1=1, R3=35, X=4, W=4, R2=14, A=50, B=58)
+LAGS = dict(P=0, S1=0, Nf=0, N=0, F=0, R1=1, R3=7, X=3, W=3, R2=42, A=56, B=56)
+CHAIN = (("C1", 15), ("C2", 23), ("C3", 47), ("C4", 19), ("Q", 48), ("QS", 53))
 ORDER = tuple(
     (kind, step - lag)
     for step in range(STEPS + max(LAGS.values()))
-    for kind, lag in LAGS.items()
-    if 0 <= step - lag < (len(GROUPS) if kind in "AB" else STEPS)
+    for kind, lag in (LAGS | dict(CHAIN)).items()
+    if 0 <= step - lag < (1 if kind in dict(CHAIN) else len(GROUPS) if kind in "AB" else STEPS)
     and (step > lag or kind not in ("P", "S1", "N", "Nf", "F"))
 )
 
@@ -97,8 +100,8 @@
 
 
 def kernel(
-    groups, taps_hbm, frames, out, taps_ref, plane, cross, relay, halo,
-    taps_sem, own_sem, row_sem, in_send, in_recv, x_recv, z_send, r_recv, h_recv,
+    groups, taps_hbm, frames, out, taps_ref, plane, cross, relay, halo, chain, part,
+    taps_sem, own_sem, row_sem, in_send, in_recv, x_recv, z_send, r_recv, h_recv, c_send, c_recv,
 ):
     g = lax.axis_index("ta")
     s = lax.axis_index("sa")
@@ -109,9 +112,15 @@
     mine = (y * NX + x) * 2 + c
     last = groups - 1
     step = 2 * a - 1
-    beyond, near = g + step, g - step
+    beyond, near = (g + step + groups) % groups, g - step
     has_near = jnp.logical_and(near >= 0, near <= last)
-    has_far = jnp.logical_and(beyond >= 0, beyond <= last)
+    has_far = jnp.logical_and(g + step >= 0, g + step <= last)
+    outer = jnp.logical_not(has_far)
+    inner = jnp.logical_not(has_near)
+    inner = jnp.logical_and(inner, has_far)
+    middle = jnp.logical_and(has_near, has_far)
+    adds = jnp.logical_and(middle, jnp.logical_or(beyond == 0, beyond == last))
+    takes = jnp.logical_and(middle, jnp.logical_not(adds))
     has_up = g < last
     has_down = g > 0
 
@@ -151,12 +160,8 @@
         yy, xx = chip(offset)
         signal(barrier, device(g, yy, a, xx, (c + other) % 2))
     signal(barrier, partner)
-
-    @pl.when(has_far)
-    def _():
-        signal(barrier, beyond_chip)
-
-    pl.semaphore_wait(barrier, len(CLOSE) + 1 + has_far.astype(jnp.int32))
+    signal(barrier, beyond_chip)
+    pl.semaphore_wait(barrier, len(CLOSE) + 2)
 
     def remote(src, dst, send, recv, target):
         return pltpu.make_async_remote_copy(
@@ -211,6 +216,34 @@
         return remote(
             relay.at[0, slots(u)], halo.at[1 - a, 0, slots(u)],
             z_send.at[6], h_recv.at[1 - a, 0, GROUP_OF[u]], beyond_chip,
+        )
+
+    def in_round(u):
+        before = ROUND[: ROUND.index(u)]
+        return pl.ds(sum(SIZES[UNITS[v][0]] for v in before), SIZES[UNITS[u][0]])
+
+    def round_copy(hop, u=None):
+        run = None if u is None else in_round(u)
+        if hop == 0:
+            return remote(
+                plane.at[slots(u), pl.ds(1 - a, 3), 1 - a], chain.at[0, run],
+                c_send, c_recv.at[0], beyond_chip,
+            )
+        if hop == 1:
+            return remote(chain.at[0], chain.at[0], c_send, c_recv.at[0], partner)
+        if hop == 2:
+            return remote(chain.at[0], chain.at[1], c_send, c_recv.at[1], beyond_chip)
+        if hop == 3:
+            return remote(chain.at[1], chain.at[1], c_send, c_recv.at[1], partner)
+        return remote(
+            chain.at[1, run], halo.at[a, 1, slots(u)],
+            c_send, h_recv.at[a, 1, GROUP_OF[u]], beyond_chip,
+        )
+
+    def part_copy(u):
+        return remote(
+            part.at[in_round(u)], cross.at[slots(u)], z_send.at[7], x_recv.at[u],
+            partner,
         )
 
     def wait_in(ref, sem):
@@ -284,20 +317,113 @@
 
         lax.fori_loop(0, run.size, body, 0)
 
+    def add_up(u):
+        def body(n, _):
+            slot, i = slots(u).start + n // 4, in_round(u).start + n // 4
+            lanes = pl.ds(pl.multiple_of(n % 4 * 128, 128), 128)
+            steps = [plane[slot, j, 1 - a, :, lanes] for j in range(4)]
+            past = [relay[2, slot, j, :, lanes] for j in range(3)]
+
+            @pl.when(a == 0)
+            def _():
+                values = past + steps
+                for t in range(4):
+                    acc = taps[0] * values[t]
+                    for j in range(1, 7 - t):
+                        acc = acc + taps[j] * values[t + j]
+                    part[i, t, :, lanes] = acc
+
+            @pl.when(a == 1)
+            def _():
+                values = steps + past
+                for t in range(4):
+                    first = max(3 - t, 0)
+                    acc = taps[first] * values[t + first - 3]
+                    for j in range(first + 1, 7):
+                        acc = acc + taps[j] * values[t + j - 3]
+                    part[i, t, :, lanes] = acc
+
+            return 0
+
+        lax.fori_loop(0, 4 * slots(u).size, body, 0)
+
+    def sum_part(u):
+        def body(n, _):
+            slot, q = slots(u).start + n // 4, n % 4
+            m = slot // 2
+            row = ((m // NX) * 2 + 1 - a) * 32 + (m % NX) * 2 + slot % 2
+            lanes = pl.ds(pl.multiple_of(q * 128, 128), 128)
+            begun = [cross[slot, t, :, lanes] for t in range(4)]
+            rest = [halo[a, 1, slot, j, :, lanes] for j in range(3)]
+
+            @pl.when(a == 1)
+            def _():
+                for t in range(4):
+                    acc = begun[t]
+                    for j in range(7 - t, 7):
+                        acc = acc + taps[j] * rest[t + j - 7]
+                    out[t, pl.ds(row + 8 * q, 8, stride=TS // 8 * 4), :] = acc
+
+            @pl.when(a == 0)
+            def _():
+                for t in range(4):
+                    acc = begun[t]
+                    for j in range(0, 3 - t):
+                        acc = acc + taps[j] * rest[t + j]
+                    out[t, pl.ds(row + 8 * q, 8, stride=TS // 8 * 4), :] = acc
+
+            return 0
+
+        lax.fori_loop(0, 4 * slots(u).size, body, 0)
+
     def finish(group, rel):
         readers = sum(SIZES[UNITS[u][0]] for u in GROUPS[group])
+        around = [u for u in GROUPS[group] if u in ROUND] if rel == 1 else []
+
+        def wait_side(side, count):
+            wait_in(halo.at[side, rel, pl.ds(0, count)], h_recv.at[side, rel, group])
+
         for side, flag in ((0, has_down), (1, has_up)):
+            if around:
+                fewer = jnp.logical_and(takes, a == 1 - side)
+
+                @pl.when(fewer)
+                def _():
+                    wait_side(side, readers - ROUND_SIZE)
+
+                flag = jnp.logical_and(flag, jnp.logical_not(fewer))
+
             @pl.when(flag)
             def _():
-                wait_in(halo.at[side, rel, pl.ds(0, readers)], h_recv.at[side, rel, group])
+                wait_side(side, readers)
+
         for u in GROUPS[group]:
-            sum_rows(u, rel)
+            if u in around:
+                @pl.when(takes)
+                def _():
+                    wait_in(cross.at[slots(u)], x_recv.at[u])
+                    sum_part(u)
+
+                @pl.when(jnp.logical_not(takes))
+                def _():
+                    sum_rows(u, rel)
+            else:
+                sum_rows(u, rel)
 
     for kind, u in ORDER:
         if kind == "P":
             wait_in(plane.at[slots(u)], in_recv.at[u])
         elif kind == "S1":
-            cross_copy(u).start()
+            if u in ROUND:
+                @pl.when(jnp.logical_not(adds))
+                def _():
+                    cross_copy(u).start()
+
+                @pl.when(adds)
+                def _():
+                    round_copy(0, u).start()
+            else:
+                cross_copy(u).start()
         elif kind == "N":
             @pl.when(has_near)
             def _():
@@ -305,11 +431,49 @@
         elif kind == "A":
             finish(u, 0)
         elif kind == "X":
-            wait_in(cross.at[slots(u)], x_recv.at[u])
+            if u in ROUND:
+                @pl.when(jnp.logical_not(takes))
+                def _():
+                    wait_in(cross.at[slots(u)], x_recv.at[u])
+            else:
+                wait_in(cross.at[slots(u)], x_recv.at[u])
+        elif kind in ("C1", "C4"):
+            @pl.when(inner)
+            def _():
+                way = 0 if kind == "C1" else 1
+                wait_in(chain.at[way], c_recv.at[way])
+                if kind == "C1":
+                    round_copy(1).start()
+                else:
+                    for v in ROUND:
+                        round_copy(4, v).start()
+        elif kind in ("C2", "C3"):
+            @pl.when(outer)
+            def _():
+                way = 0 if kind == "C2" else 1
+                wait_in(chain.at[way], c_recv.at[way])
+                round_copy(2 + way).start()
+        elif kind == "Q":
+            @pl.when(adds)
+            def _():
+                for v in ROUND:
+                    wait_in(relay.at[2, slots(v)], r_recv.at[2, v])
+                    add_up(v)
+        elif kind == "QS":
+            @pl.when(adds)
+            def _():
+                for v in ROUND:
+                    part_copy(v).start()
         elif kind == "B":
             finish(u, 1)
         else:
-            @pl.when(has_far)
+            flag = has_far
+            if u in ROUND and kind == "W":
+                flag = jnp.logical_and(flag, jnp.logical_not(takes))
+            if u in ROUND and kind == "R2":
+                flag = jnp.logical_and(flag, jnp.logical_not(middle))
+
+            @pl.when(flag)
             def _():
                 if kind == "Nf":
                     far_halo(u).start()
@@ -334,10 +498,29 @@
     def _():
         wait_out(relay.at[0], z_send.at[0])
 
+    few = SLOTS - ROUND_SIZE
+
     @pl.when(has_far)
     def _():
-        for kind in range(1, 7):
+        for kind in (1, 2, 4, 6):
             wait_out(relay.at[0], z_send.at[kind])
+
+        for kind, fewer in ((3, takes), (5, middle)):
+            @pl.when(fewer)
+            def _():
+                wait_out(relay.at[0, pl.ds(0, few)], z_send.at[kind])
+
+            @pl.when(jnp.logical_not(fewer))
+            def _():
+                wait_out(relay.at[0], z_send.at[kind])
+
+    @pl.when(adds)
+    def _():
+        wait_out(chain.at[0], c_send)
+
+    @pl.when(jnp.logical_or(inner, outer))
+    def _():
+        wait_out(chain, c_send)
 
 
 def on_device(groups, frames, taps):
@@ -353,6 +536,8 @@
             pltpu.VMEM((SLOTS, 4, 8, TS), jnp.float32),
             pltpu.VMEM((3, SLOTS, 3, 8, TS), jnp.float32),
             pltpu.VMEM((2, 2, SLOTS, 3, 8, TS), jnp.float32),
+            pltpu.VMEM((2, ROUND_SIZE, 3, 8, TS), jnp.float32),
+            pltpu.VMEM((ROUND_SIZE, 4, 8, TS), jnp.float32),
             pltpu.SemaphoreType.DMA,
             pltpu.SemaphoreType.DMA,
             pltpu.SemaphoreType.REGULAR,
@@ -362,6 +547,8 @@
             pltpu.SemaphoreType.DMA((8,)),
             pltpu.SemaphoreType.DMA((3, STEPS)),
             pltpu.SemaphoreType.DMA((2, 2, len(GROUPS))),
+            pltpu.SemaphoreType.DMA,
+            pltpu.SemaphoreType.DMA((2,)),
         ],
         compiler_params=pltpu.CompilerParams(
             collective_id=0, has_side_effects=True, vmem_limit_bytes=24 * 2**20

time: 156 us -> 152 us (0.974)
  Pallas kernels: 154 us -> 150 us
    pallas_call x1, Pallas kernels: 154 us -> 150 us  [on_device(): pl.pallas_call(functools.partial(kernel, groups), out_shape=jax.ShapeDtyp...]
where the time goes in v4:
time: 152 us
  Pallas kernels  150 us (99%)
  local copies, waits for them, and re-layouts  2.02 us (1%)
    pallas_call x1, Pallas kernels, on_device(): pl.pallas_call(functools.partial(kernel, groups), out_shape=jax.ShapeDtyp...  150 us

profile of v4, /device:TPU:64, one launch (start us, length us, event | category | flops | bytes accessed | tf_op | source)
XLA Modules:
  0.0 151.7 jit_solution(65085057105455635)
XLA Ops:
  0.0 149.7 %exchange.1 = f32[4,2048,128]{2,1,0:T(8,128)S(1)} custom-call(f32[7]{0:T(128)} %taps_hbm.1, f32[4,8,8,4096]{3,2,1,0:T(8,128)} %bitcast.7), custom_call_target="tpu_custom_call" | custom-call | tf_op jit(solution)/shard_map/exchange/pallas_call | solution.py:528
  149.7 2.0 %copy.4 = f32[1,4,512,512]{3,2,1,0:T(8,128)} copy(f32[1,4,512,512]{3,2,1,0:T(8,128)S(1)} %bitcast.6) | data formatting | bytes 8388608

commit v5 on v4

--- a/solution.py
+++ b/solution.py
@@ -69,7 +69,7 @@
 SIZES = {"one": 1, "chip": 2, "pair": 4}
 STEPS = len(UNITS)
 GROUPS = (tuple(range(2, 10)), (0, 1, 10, 11), (12, 13), (14,), (15,), (16,))
-ROUND = (13,)
+ROUND = (9, 13)
 ROUND_SIZE = sum(SIZES[UNITS[u][0]] for u in ROUND)
 GROUP_OF = {u: i for i, units in enumerate(GROUPS) for u in units}
 LAGS = dict(P=0, S1=0, Nf=0, N=0, F=0, R1=1, R3=7, X=3, W=3, R2=42, A=56, B=56)
@@ -389,7 +389,7 @@
 
                 @pl.when(fewer)
                 def _():
-                    wait_side(side, readers - ROUND_SIZE)
+                    wait_side(side, readers - sum(SIZES[UNITS[u][0]] for u in around))
 
                 flag = jnp.logical_and(flag, jnp.logical_not(fewer))
 

time: 152 us -> 151 us (level)
  no operation moved by 1% of the time
where the time goes in v5:
time: 151 us
  Pallas kernels  149 us (99%)
  local copies, waits for them, and re-layouts  2.02 us (1%)
    pallas_call x1, Pallas kernels, on_device(): pl.pallas_call(functools.partial(kernel, groups), out_shape=jax.ShapeDtyp...  149 us

profile of v5, /device:TPU:64, one launch (start us, length us, event | category | flops | bytes accessed | tf_op | source)
XLA Modules:
  0.0 150.7 jit_solution(13229259725617324877)
XLA Ops:
  0.0 148.6 %exchange.1 = f32[4,2048,128]{2,1,0:T(8,128)S(1)} custom-call(f32[7]{0:T(128)} %taps_hbm.1, f32[4,8,8,4096]{3,2,1,0:T(8,128)} %bitcast.7), custom_call_target="tpu_custom_call" | custom-call | tf_op jit(solution)/shard_map/exchange/pallas_call | solution.py:528
  148.6 2.0 %copy.4 = f32[1,4,512,512]{3,2,1,0:T(8,128)} copy(f32[1,4,512,512]{3,2,1,0:T(8,128)S(1)} %bitcast.6) | data formatting | bytes 8388608

commit v6 on v5

--- a/solution.py
+++ b/solution.py
@@ -72,7 +72,7 @@
 ROUND = (9, 13)
 ROUND_SIZE = sum(SIZES[UNITS[u][0]] for u in ROUND)
 GROUP_OF = {u: i for i, units in enumerate(GROUPS) for u in units}
-LAGS = dict(P=0, S1=0, Nf=0, N=0, F=0, R1=1, R3=7, X=3, W=3, R2=42, A=56, B=56)
+LAGS = dict(P=0, S1=0, Nf=0, N=0, F=0, R1=1, R3=7, X=3, W=3, R2=42, A=59, B=59)
 CHAIN = (("C1", 15), ("C2", 23), ("C3", 47), ("C4", 19), ("Q", 48), ("QS", 53))
 ORDER = tuple(
     (kind, step - lag)

time: 151 us -> 151 us (level)
  no operation moved by 1% of the time
where the time goes in v6:
time: 151 us
  Pallas kernels  149 us (99%)
  local copies, waits for them, and re-layouts  2.02 us (1%)
    pallas_call x1, Pallas kernels, on_device(): pl.pallas_call(functools.partial(kernel, groups), out_shape=jax.ShapeDtyp...  149 us

profile of v6, /device:TPU:64, one launch (start us, length us, event | category | flops | bytes accessed | tf_op | source)
XLA Modules:
  0.0 150.7 jit_solution(15079800492195825088)
XLA Ops:
  0.0 148.6 %exchange.1 = f32[4,2048,128]{2,1,0:T(8,128)S(1)} custom-call(f32[7]{0:T(128)} %taps_hbm.1, f32[4,8,8,4096]{3,2,1,0:T(8,128)} %bitcast.7), custom_call_target="tpu_custom_call" | custom-call | tf_op jit(solution)/shard_map/exchange/pallas_call | solution.py:528
  148.6 2.0 %copy.4 = f32[1,4,512,512]{3,2,1,0:T(8,128)} copy(f32[1,4,512,512]{3,2,1,0:T(8,128)S(1)} %bitcast.6) | data formatting | bytes 8388608
